TPU v7x, 32 devices: a whole 2x2x4 slice. The times are simulated.
32 devices in a mesh: band: 8 (over z, core), lane: 4 (over y, x).
Axes of the slice: x: 2, y: 2, z: 4, core: 2. Of those that a mesh axis runs over, the one named last changes fastest.
Arguments:
- first_factor: bfloat16 [8192, 4096], P('band', 'lane'), may hold values from -6 to 6
- second_factor: bfloat16 [4096, 2048], P('band', 'lane'), may hold values from -0.09375 to 0.09375
- result_in: float32 [8192, 2048], P('band', 'lane'), may hold values from -6 to 6
- pivot_scale: float32 [4096], replicated, may hold values from 0.25 to 1.75
Outputs:
- updated: float32 [8192, 2048], P('band', 'lane')
All inputs are finite; a program needn't handle non-finite values.
Results may differ from a plain program's by a relative error of at most 0.002.
Values may be sent and summed in bfloat16 or wider, within the bound.
A program may use at most 128 MiB of HBM per device.

v0:
```python
import jax
import jax.numpy as jnp
from jax import lax
from jax.sharding import PartitionSpec as P


def join_panel(left_panel, right_panel):
    return jnp.dot(left_panel, right_panel, preferred_element_type=jnp.float32)


def on_device(first_factor, second_factor, result_in, pivot_scale):
    share = first_factor.shape[1]
    part_scale = lax.dynamic_slice_in_dim(pivot_scale, lax.axis_index("lane") * share, share)
    scaled_left = (first_factor.astype(jnp.float32) * part_scale).astype(jnp.bfloat16)
    left_line = lax.all_gather(scaled_left, "lane", axis=1, tiled=True)
    total = join_panel(left_line, lax.all_gather(second_factor, "band", axis=0, tiled=True))
    updated = result_in - total
    row_power = lax.psum(jnp.sum(updated * updated, axis=1), "lane")
    updated = (
        updated * lax.rsqrt(row_power / (updated.shape[1] * lax.axis_size("lane")) + 1e-06)[:, None]
    )
    return updated


def solution(mesh):
    return jax.shard_map(
        on_device,
        mesh=mesh,
        in_specs=(P("band", "lane"), P("band", "lane"), P("band", "lane"), P()),
        out_specs=P("band", "lane"),
        check_vma=False,
    )
```

profile of v0, /device:TPU:0, one launch (start us, length us, event | category | flops | bytes accessed | tf_op | source)
XLA Modules:
  0.0 177.2 jit_solution(5245780658395474004)
XLA Ops:
  6.5 0.0 all-gather.5.cloned.1.call-start
  6.5 0.7 all-gather.5.cloned.1.call-update
  7.3 0.0 all-gather.3.cloned.1.call-start
  7.3 0.7 dynamic_slice.3
  8.0 3.5 %multiply_convert_fusion = bf16[1024,1024]{1,0:T(8,128)(2,1)} fusion(bf16[1024,1024]{1,0:T(8,128)(2,1)} %param.4, f32[1024]{0:T(1024)S(1)} %dynamic_slice.3), kind=kLoop, calls=%fused_computation | loop fusion | flops 3145728 | bytes 4198400 | tf_op jit(solution)/shard_map/convert_element_type | solution.py:14
  11.5 0.0 copy-start
  11.5 0.0 all-gather.3.cloned.1.call-update
  11.5 1.6 copy-done
  13.1 1.8 %copy.5 = f32[1024,512]{0,1:T(8,128)} copy(f32[1024,512]{1,0:T(8,128)S(1)} %copy-done) | data formatting | bytes 4194304 | tf_op args[2]
  14.9 43.7 %all-gather.5.cloned.1.call-done = bf16[4096,512]{1,0:T(8,128)(2,1)} async-done(((bf16[512,512]{1,0:T(8,128)(2,1)}), bf16[4096,512]{1,0:T(8,128)(2,1)}) %all-gather.5.cloned.1.call-update) | async-done | bytes 4194320 | tf_op jit(solution)/shard_map/all_gather | solution.py:16
  58.6 88.2 %all-gather.3.cloned.1.call-done = bf16[1024,4096]{1,0:T(8,128)(2,1)} async-done(((bf16[1024,1024]{1,0:T(8,128)(2,1)}), bf16[1024,4096]{1,0:T(8,128)(2,1)}) %all-gather.3.cloned.1.call-update) | async-done | bytes 8388624 | tf_op jit(solution)/shard_map/all_gather | solution.py:15
  146.7 11.1 %multiply_reduce_fusion = (f32[1024]{0:T(1024)S(1)}, f32[1024,512]{0,1:T(8,128)}) fusion(f32[1024,512]{0,1:T(8,128)} %copy.5, bf16[1024,4096]{1,0:T(8,128)(2,1)} %all-gather.3.cloned.1.call-done, bf16[4096,512]{1,0:T(8,128)(2,1)} %all-gather.5.cloned.1.call-done), kind=kOutput, calls=%fused_computation.1 | convolution fusion | flops 4296539136 | bytes 16781312 | tf_op jit(solution)/shard_map/dot_general | solution.py:8
  157.8 8.9 %psum.7 = f32[1024]{0:T(1024)S(1)} all-reduce(f32[1024]{0:T(1024)S(1)} %get-tuple-element.5), channel_id=1, replica_groups=mesh['band'=8,'lane'=4] {'lane'}, use_global_device_ids=true, to_apply=%region_1.0 | all-reduce | flops 1024 | bytes 8192 | tf_op jit(solution)/shard_map/psum | solution.py:18
  166.7 1.8 %broadcast_multiply_fusion = f32[1024,512]{0,1:T(8,128)S(1)} fusion(f32[1024,512]{0,1:T(8,128)} %get-tuple-element.6, f32[1024]{0:T(1024)S(1)} %add_rsqrt_fusion), kind=kLoop, calls=%fused_computation.3 | loop fusion | flops 524288 | bytes 4198400 | tf_op jit(solution)/shard_map/mul | solution.py:20
  168.6 1.8 %copy.6 = f32[1024,512]{1,0:T(8,128)} copy(f32[1024,512]{0,1:T(8,128)S(1)} %broadcast_multiply_fusion) | data formatting | bytes 4194304 | tf_op jit(solution)/shard_map/mul | solution.py:20
  (1 shorter events, 0.0 us)
Async XLA Ops:
  6.5 52.0 %all-gather.5.cloned.1.call-start = ((), (), s32[]{:S(2)}) async-start(), calls=%async_computation.1 | async-start | bytes 4718592 | tf_op jit(solution)/shard_map/all_gather | solution.py:16
  7.3 139.5 %all-gather.3.cloned.1.call-start = ((), (), s32[]{:S(2)}) async-start(), calls=%async_computation | async-start | bytes 10485760 | tf_op jit(solution)/shard_map/all_gather | solution.py:15
  11.5 1.6 copy-start
Sparse Core Ops, SparseCore 0:
  8.9 49.5 all-gather.4
  60.4 86.2 all-gather.2
where the time goes:
time: 177 us
  waiting for transfers between devices  133 us (75%)
  between operations  13.4 us (8%)
  matrix products  11.1 us (6%)
  blocking collectives  8.9 us (5%)
  local copies, waits for them, and re-layouts  5.88 us (3%)
  other arithmetic  5.32 us (3%)
    all_gather x1, waiting for transfers between devices, on_device(): left_line = lax.all_gather(scaled_left, 'lane', axis=1, tiled=True)  88.2 us
    all_gather x1, waiting for transfers between devices, on_device(): lax.all_gather(second_factor, 'band', axis=0, tiled=True)  43.7 us
    dot_general x1, matrix products, join_panel(): return jnp.dot(left_panel, right_panel, preferred_element_type=jnp.float32)  11.1 us
    psum x1, blocking collectives, on_device(): row_power = lax.psum(jnp.sum(updated * updated, axis=1), 'lane')  8.9 us
  transfers between devices with their start and end apart: 2, of which 2 were waited for; matrix products, arithmetic and copies ran while one was open for 3% of the time, Pallas kernels for 0%

commit v1 on v0

v1 whole, which is shorter than its diff:
```python
import functools

import jax
import jax.numpy as jnp
from jax import lax
from jax.experimental import pallas as pl
from jax.experimental.pallas import tpu as pltpu
from jax.sharding import PartitionSpec as P

MESH = pl.DeviceIdType.MESH
PIECES = 2
TILES = 4


def gathered(first_factor, second_factor, result_in, pivot_scale):
    share = first_factor.shape[1]
    part_scale = lax.dynamic_slice_in_dim(pivot_scale, lax.axis_index("lane") * share, share)
    scaled_left = (first_factor.astype(jnp.float32) * part_scale).astype(jnp.bfloat16)
    left_line = lax.all_gather(scaled_left, "lane", axis=1, tiled=True)
    right = lax.all_gather(second_factor, "band", axis=0, tiled=True)
    updated = result_in - jnp.dot(left_line, right, preferred_element_type=jnp.float32)
    row_power = lax.psum(jnp.sum(updated * updated, axis=1), "lane")
    return (
        updated * lax.rsqrt(row_power / (updated.shape[1] * lax.axis_size("lane")) + 1e-06)[:, None]
    )


def kernel(
    chips, left_hbm, right_hbm, result_hbm, scale_ref, out_ref, power_ref,
    left_raw, left, right, result, outgoing, incoming, kept, norm_out, norm_in,
    load_sem, source_sem, right_sem, up_sem, down_sem, peer_send, peer_recv, part_send, part_recv,
    norm_send, norm_recv,
):
    band, lane = lax.axis_index("band"), lax.axis_index("lane")
    z, core = band // 2, band % 2
    y, x = lane // 2, lane % 2
    peer = (2 * z + 1 - core, lane)
    lane_x, lane_y, lane_d = 2 * y + 1 - x, 2 * (1 - y) + x, 2 * (1 - y) + 1 - x
    above, below = (band + 2, lane), (band - 2, lane)
    depth, width = right_hbm.shape
    half = width // 2
    piece = depth // PIECES
    rows, share = left.shape
    tile = rows // TILES

    load_left = pltpu.make_async_copy(left_hbm, left_raw, load_sem.at[0])
    load_left.start()
    load_result = pltpu.make_async_copy(result_hbm, result, load_sem.at[1])
    load_result.start()

    barrier = pltpu.get_barrier_semaphore()
    for other in (lane_x, lane_y, lane_d):
        pl.semaphore_signal(barrier, inc=1, device_id=(band, other), device_id_type=MESH)
    pl.semaphore_signal(barrier, inc=1, device_id=peer, device_id_type=MESH)

    @pl.when(z < chips - 1)
    def _():
        pl.semaphore_signal(barrier, inc=1, device_id=above, device_id_type=MESH)

    @pl.when(z > 0)
    def _():
        pl.semaphore_signal(barrier, inc=1, device_id=below, device_id_type=MESH)

    pl.semaphore_wait(barrier, 4 + (z + chips - 1) // chips + (2 * chips - 2 - z) // chips)

    def place(slot, part, of_core):
        start = pl.multiple_of(of_core * depth + part * piece, piece)
        return right.at[slot, pl.ds(start, piece), :]

    dx, dy = (x + z % 2) % 2, (y + z // 2) % 2
    slot_0 = 4 * dx * (1 - dy) + 3 * (1 - dx) * dy + 6 * (1 - dx) * (1 - dy)
    slot_1 = dx * dy + 2 * dx * (1 - dy) + 5 * (1 - dx) * dy + 7 * (1 - dx) * (1 - dy)

    def own_block(i, part):
        side = (i + dx * (1 - dy)) % 2
        slot = slot_0 * (1 - side) + slot_1 * side
        block = right_hbm.at[
            pl.ds(part * piece, piece), pl.ds(pl.multiple_of(side * half, half), half)
        ]
        return block, slot

    def send_own(i, part):
        block, slot = own_block(i, part)
        return pltpu.make_async_remote_copy(
            block, place(slot, part, core), source_sem.at[i * PIECES + part],
            right_sem.at[slot * PIECES + part], device_id=(band, z), device_id_type=MESH,
        )

    @pl.when(lane != z)
    def _():
        for i in range(2):
            for part in range(PIECES):
                send_own(i, part).start()

    @pl.when(lane == z)
    def _():
        for i in range(2):
            for part in range(PIECES):
                block, slot = own_block(i, part)
                pltpu.make_async_copy(
                    block, place(slot, part, core), right_sem.at[slot * PIECES + part]
                ).start()

    def along(slot, part, device, send, recv):
        at = slot * PIECES + part
        ref = place(slot, part, core)
        return pltpu.make_async_remote_copy(
            ref, ref, send.at[at], recv.at[at], device_id=device, device_id_type=MESH
        )

    def forward(slot):
        for part in range(PIECES):
            along(slot, part, peer, peer_send, right_sem).wait_recv()

            @pl.when((z >= lane) & (z < chips - 1))
            def _():
                along(slot, part, above, up_sem, right_sem).start()

            @pl.when((z <= lane) & (z > 0))
            def _():
                along(slot, part, below, down_sem, right_sem).start()

            along(slot, part, peer, peer_send, peer_recv).start()

    def await_peer(slot):
        for part in range(PIECES):
            at = slot * PIECES + part
            ref = place(slot, part, 1 - core)
            pltpu.make_async_remote_copy(
                ref, ref, peer_send.at[at], peer_recv.at[at], device_id=peer, device_id_type=MESH
            ).wait_recv()

    def part_copy(buffer, at, other):
        index = buffer * TILES + at
        span = pl.ds(pl.multiple_of(at * tile, tile), tile)
        return pltpu.make_async_remote_copy(
            outgoing.at[buffer, span, :], incoming.at[buffer, span, :], part_send.at[index],
            part_recv.at[index], device_id=(band, other), device_id_type=MESH,
        )

    def product(slot, span):
        return jnp.dot(left[span, :], right[slot], preferred_element_type=jnp.float32)

    def each_tile(body):
        @pl.loop(0, TILES)
        def _(at):
            body(at, pl.ds(pl.multiple_of(at * tile, tile), tile))

    def multiply_send(slot, buffer, other):
        def body(at, span):
            outgoing[buffer, span, :] = product(slot, span).astype(jnp.bfloat16)
            part_copy(buffer, at, other).start()

        each_tile(body)

    def multiply_keep(slot, which):
        def body(at, span):
            kept[which, span, :] = product(slot, span)

        each_tile(body)

    def combine_send(which, arrived, buffer, other):
        def body(at, span):
            part_copy(arrived, at, other).wait_recv()
            total = kept[which, span, :] + incoming[arrived, span, :].astype(jnp.float32)
            outgoing[buffer, span, :] = total.astype(jnp.bfloat16)
            part_copy(buffer, at, other).start()

        each_tile(body)

    def multiply_own(slot, side):
        def body(at, span):
            columns = slice(side * half, (side + 1) * half)
            out_ref[span, columns] = result[span, columns] - product(slot, span)

        each_tile(body)

    load_left.wait()
    part_scale = scale_ref[:, pl.ds(pl.multiple_of(lane * share, share), share)]

    def scale_tile(at, span):
        left[span, :] = (left_raw[span, :].astype(jnp.float32) * part_scale).astype(jnp.bfloat16)

    each_tile(scale_tile)

    forward(0)
    await_peer(0)
    multiply_send(0, 0, lane_x)
    forward(1)
    await_peer(1)
    multiply_send(1, 1, lane_y)
    forward(2)
    await_peer(2)
    multiply_keep(2, 0)
    forward(3)
    await_peer(3)
    multiply_keep(3, 1)
    forward(4)
    await_peer(4)
    multiply_send(4, 2, lane_x)
    forward(5)
    await_peer(5)
    multiply_send(5, 3, lane_y)
    forward(6)
    combine_send(0, 1, 4, lane_x)
    combine_send(1, 0, 5, lane_y)
    forward(7)
    load_result.wait()
    await_peer(6)
    multiply_own(6, 0)
    await_peer(7)
    multiply_own(7, 1)

    def finish(at, span):
        for buffer in (2, 3, 4, 5):
            part_copy(buffer, at, lane_x).wait_recv()
        first = out_ref[span, :half] - (
            incoming[2, span, :].astype(jnp.float32) + incoming[5, span, :].astype(jnp.float32)
        )
        second = out_ref[span, half:] - (
            incoming[3, span, :].astype(jnp.float32) + incoming[4, span, :].astype(jnp.float32)
        )
        out_ref[span, :half] = first
        out_ref[span, half:] = second
        power = first * first + second * second
        power = sum(power[:, k : k + 128] for k in range(0, half, 128))
        norm_out[:, span] = jnp.sum(power.T.reshape(16, 8, tile), axis=0)

    each_tile(finish)

    norms = [
        pltpu.make_async_remote_copy(
            norm_out, norm_in.at[k], norm_send.at[k], norm_recv.at[k],
            device_id=(band, other), device_id_type=MESH,
        )
        for k, other in enumerate((lane_x, lane_y, lane_d))
    ]
    for copy in norms:
        copy.start()

    @pl.when(lane != z)
    def _():
        for i in range(2):
            for part in range(PIECES):
                send_own(i, part).wait_send()

    for slot in range(8):
        for part in range(PIECES):
            along(slot, part, peer, peer_send, peer_recv).wait_send()

    @pl.when((z >= lane) & (z < chips - 1))
    def _():
        for slot in range(8):
            for part in range(PIECES):
                along(slot, part, above, up_sem, right_sem).wait_send()

    @pl.when((z <= lane) & (z > 0))
    def _():
        for slot in range(8):
            for part in range(PIECES):
                along(slot, part, below, down_sem, right_sem).wait_send()

    for buffer in range(6):
        for at in range(TILES):
            part_copy(buffer, at, lane_x).wait_send()

    for copy in norms:
        copy.wait()
    power = norm_out[...] + norm_in[0] + norm_in[1] + norm_in[2]
    power = jnp.sum(power, axis=0, keepdims=True)
    power_ref[...] = jnp.broadcast_to(power, (128, rows)).T


def on_device(chips, first_factor, second_factor, result_in, pivot_scale):
    rows, share = first_factor.shape
    depth, width = second_factor.shape
    half = width // 2
    slots = 8 * PIECES
    dma = pltpu.SemaphoreType.DMA
    flops = 2 * rows * share * 4 * width
    updated, power = pl.pallas_call(
        functools.partial(kernel, chips),
        out_shape=(
            jax.ShapeDtypeStruct((rows, width), jnp.float32),
            jax.ShapeDtypeStruct((rows, 128), jnp.float32),
        ),
        in_specs=[pl.BlockSpec(memory_space=pl.ANY)] * 3
        + [pl.BlockSpec(memory_space=pltpu.VMEM)],
        out_specs=[pl.BlockSpec(memory_space=pltpu.VMEM)] * 2,
        scratch_shapes=[
            pltpu.VMEM((rows, share), jnp.bfloat16),
            pltpu.VMEM((rows, share), jnp.bfloat16),
            pltpu.VMEM((8, share, half), jnp.bfloat16),
            pltpu.VMEM((rows, width), jnp.float32),
            pltpu.VMEM((6, rows, half), jnp.bfloat16),
            pltpu.VMEM((6, rows, half), jnp.bfloat16),
            pltpu.VMEM((2, rows, half), jnp.float32),
            pltpu.VMEM((8, rows), jnp.float32),
            pltpu.VMEM((3, 8, rows), jnp.float32),
            dma((2,)),
            dma((2 * PIECES,)),
            dma((slots,)),
            dma((slots,)),
            dma((slots,)),
            dma((slots,)),
            dma((slots,)),
            dma((6 * TILES,)),
            dma((6 * TILES,)),
            dma((3,)),
            dma((3,)),
        ],
        compiler_params=pltpu.CompilerParams(
            collective_id=0, has_side_effects=True, vmem_limit_bytes=48 * 1024 * 1024
        ),
        cost_estimate=pl.CostEstimate(
            flops=flops, bytes_accessed=8 * rows * share, transcendentals=0
        ),
    )(first_factor, second_factor, result_in, pivot_scale.reshape(1, -1))
    return updated * lax.rsqrt(power[:, :1] / (width * lax.axis_size("lane")) + 1e-06)


def solution(mesh):
    bands, lanes = mesh.shape["band"], mesh.shape["lane"]

    def body(first_factor, second_factor, result_in, pivot_scale):
        fits = lanes == 4 and bands == 2 * lanes
        plan = functools.partial(on_device, bands // 2) if fits else gathered
        return plan(first_factor, second_factor, result_in, pivot_scale)

    return jax.shard_map(
        body,
        mesh=mesh,
        in_specs=(P("band", "lane"), P("band", "lane"), P("band", "lane"), P()),
        out_specs=P("band", "lane"),
        check_vma=False,
    )
```

time: 177 us -> 93.1 us (0.53)
  waiting for transfers between devices: 133 us -> 0 us
  Pallas kernels: 0 us -> 87.7 us
  between operations: 13.4 us -> 0.02 us
  matrix products: 11.1 us -> 0 us
  blocking collectives: 8.9 us -> 0 us
  other arithmetic: 5.32 us -> 1.74 us
  local copies, waits for them, and re-layouts: 5.88 us -> 3.35 us
    all_gather x2 -> x0, waiting for transfers between devices: 132 us -> none  [the longest x1 88.2 us: on_device(): left_line = lax.all_gather(scaled_left, 'lane', axis=1, tiled=True)]
    pallas_call x0 -> x1, Pallas kernels: none -> 87.7 us  [on_device(): pl.pallas_call(functools.partial(kernel, chips), out_shape=(jax.ShapeDtyp...]
    dot_general x1 -> x0, matrix products: 11.1 us -> none  [join_panel(): return jnp.dot(left_panel, right_panel, preferred_element_type=jnp.float32)]
    psum x1 -> x0, blocking collectives: 8.9 us -> none  [on_device(): row_power = lax.psum(jnp.sum(updated * updated, axis=1), 'lane')]
    convert_element_type x1 -> x0, other arithmetic: 3.49 us -> none  [on_device(): (first_factor.astype(jnp.float32) * part_scale).astype(jnp.bfloat16)]
    mul x1 -> x0, local copies, waits for them, and re-layouts: 1.81 us -> none  [on_device(): updated * lax.rsqrt(row_power / (updated.shape[1] * lax.axis_size('lane')...]
  transfers between devices with their start and end apart: 2 -> 0, of which waited for: 2 -> 0; matrix products, arithmetic and copies ran while one was open for 3% -> 0% of each run, Pallas kernels for 0% -> 0%
where the time goes in v1:
time: 93.1 us; the launch traced here: 92.9 us
  Pallas kernels  87.7 us (94%)
  local copies, waits for them, and re-layouts  3.35 us (4%)
  other arithmetic  1.74 us (2%)
    pallas_call x1, Pallas kernels, on_device(): pl.pallas_call(functools.partial(kernel, chips), out_shape=(jax.ShapeDtyp...  87.7 us
    unnamed x6, local copies, waits for them, and re-layouts  3.35 us

profile of v1, /device:TPU:0, one launch (start us, length us, event | category | flops | bytes accessed | tf_op | source)
XLA Modules:
  0.0 92.9 jit_solution(10571036303215023542)
XLA Ops:
  0.0 0.0 copy-start
  0.0 1.6 %copy-done = bf16[1024,1024]{1,0:T(8,128)(2,1)S(1)} copy-done((bf16[1024,1024]{1,0:T(8,128)(2,1)S(1)}, bf16[1024,1024]{1,0:T(8,128)(2,1)}, u32[]{:S(2)}) %copy-start) | copy-done | bytes 2097176
  1.6 0.0 copy-start.1
  1.6 1.0 %copy-done.1 = bf16[512,512]{1,0:T(8,128)(2,1)S(1)} copy-done((bf16[512,512]{1,0:T(8,128)(2,1)S(1)}, bf16[512,512]{1,0:T(8,128)(2,1)}, u32[]{:S(2)}) %copy-start.1) | copy-done | bytes 524312
  2.6 0.0 copy-start.2
  2.6 0.7 copy-done.2
  3.4 87.7 %shard_map.46 = (f32[1024,512]{1,0:T(8,128)S(1)}, f32[1024,128]{1,0:T(8,128)S(1)}) custom-call(bf16[1024,1024]{1,0:T(8,128)(2,1)S(1)} %copy-done, bf16[512,512]{1,0:T(8,128)(2,1)S(1)} %copy-done.1, f32[1024,512]{1,0:T(8,128)} %result_hbm.1, f32[1,4096]{1,0:T(1,128)S(1)} %bitcast.1), custom_call_target="tpu_custom_call" | custom-call | flops 4294967296 | bytes 8388608 | tf_op jit(solution)/shard_map/pallas_call | solution.py:281
  91.1 0.2 rsqrt_reduce_fusion
  91.3 1.5 %broadcast_multiply_fusion = f32[1024,512]{1,0:T(8,128)} fusion(f32[1024,512]{1,0:T(8,128)S(1)} %get-tuple-element.7, f32[1024]{0:T(1024)S(1)} %rsqrt_reduce_fusion), kind=kLoop, calls=%fused_computation | loop fusion | flops 524288 | bytes 4198400 | tf_op jit(solution)/shard_map/mul | solution.py:319
Async XLA Ops:
  0.0 1.6 %copy-start = (bf16[1024,1024]{1,0:T(8,128)(2,1)S(1)}, bf16[1024,1024]{1,0:T(8,128)(2,1)}, u32[]{:S(2)}) copy-start(bf16[1024,1024]{1,0:T(8,128)(2,1)} %left_hbm.1) | copy-start | bytes 6291460
  1.6 1.0 %copy-start.1 = (bf16[512,512]{1,0:T(8,128)(2,1)S(1)}, bf16[512,512]{1,0:T(8,128)(2,1)}, u32[]{:S(2)}) copy-start(bf16[512,512]{1,0:T(8,128)(2,1)} %right_hbm.1) | copy-start | bytes 1572868
  2.6 0.7 copy-start.2

commit v2 on v1

--- a/solution.py
+++ b/solution.py
@@ -8,8 +8,11 @@
 from jax.sharding import PartitionSpec as P
 
 MESH = pl.DeviceIdType.MESH
-PIECES = 2
+PIECES = 4
 TILES = 4
+SWAP = 0
+EARLY = 1
+VMEM = 48 * 1024 * 1024
 
 
 def gathered(first_factor, second_factor, result_in, pivot_scale):
@@ -36,6 +39,8 @@
     y, x = lane // 2, lane % 2
     peer = (2 * z + 1 - core, lane)
     lane_x, lane_y, lane_d = 2 * y + 1 - x, 2 * (1 - y) + x, 2 * (1 - y) + 1 - x
+    if SWAP:
+        lane_x, lane_y = lane_y, lane_x
     above, below = (band + 2, lane), (band - 2, lane)
     depth, width = right_hbm.shape
     half = width // 2
@@ -68,11 +73,13 @@
         return right.at[slot, pl.ds(start, piece), :]
 
     dx, dy = (x + z % 2) % 2, (y + z // 2) % 2
-    slot_0 = 4 * dx * (1 - dy) + 3 * (1 - dx) * dy + 6 * (1 - dx) * (1 - dy)
-    slot_1 = dx * dy + 2 * dx * (1 - dy) + 5 * (1 - dx) * dy + 7 * (1 - dx) * (1 - dy)
+    if SWAP:
+        dx, dy = dy, dx
+    slot_0 = dx * (1 - dy) + 6 * (1 - dx) * dy + 4 * dx * dy
+    slot_1 = 7 * (1 - dx) * (1 - dy) + 5 * dx * (1 - dy) + 3 * (1 - dx) * dy + 2 * dx * dy
 
     def own_block(i, part):
-        side = (i + dx * (1 - dy)) % 2
+        side = (i + dy) % 2
         slot = slot_0 * (1 - side) + slot_1 * side
         block = right_hbm.at[
             pl.ds(part * piece, piece), pl.ds(pl.multiple_of(side * half, half), half)
@@ -185,31 +192,37 @@
 
     forward(0)
     await_peer(0)
-    multiply_send(0, 0, lane_x)
+    load_result.wait()
+    multiply_own(0, 0)
     forward(1)
     await_peer(1)
-    multiply_send(1, 1, lane_y)
+    multiply_send(1, 2, lane_x)
     forward(2)
     await_peer(2)
-    multiply_keep(2, 0)
+    multiply_send(2, 1, lane_y)
     forward(3)
     await_peer(3)
-    multiply_keep(3, 1)
+    multiply_send(3, 3, lane_y)
     forward(4)
     await_peer(4)
-    multiply_send(4, 2, lane_x)
+    multiply_send(4, 0, lane_x)
     forward(5)
     await_peer(5)
-    multiply_send(5, 3, lane_y)
+    multiply_keep(5, 0)
     forward(6)
+    await_peer(6)
+    multiply_keep(6, 1)
     combine_send(0, 1, 4, lane_x)
-    combine_send(1, 0, 5, lane_y)
-    forward(7)
-    load_result.wait()
-    await_peer(6)
-    multiply_own(6, 0)
-    await_peer(7)
-    multiply_own(7, 1)
+    if EARLY:
+        combine_send(1, 0, 5, lane_y)
+        forward(7)
+        await_peer(7)
+        multiply_own(7, 1)
+    else:
+        forward(7)
+        combine_send(1, 0, 5, lane_y)
+        await_peer(7)
+        multiply_own(7, 1)
 
     def finish(at, span):
         for buffer in (2, 3, 4, 5):
@@ -310,7 +323,7 @@
             dma((3,)),
         ],
         compiler_params=pltpu.CompilerParams(
-            collective_id=0, has_side_effects=True, vmem_limit_bytes=48 * 1024 * 1024
+            collective_id=0, has_side_effects=True, vmem_limit_bytes=VMEM
         ),
         cost_estimate=pl.CostEstimate(
             flops=flops, bytes_accessed=8 * rows * share, transcendentals=0

time: 93.1 us -> 81.9 us (0.88)
  Pallas kernels: 87.7 us -> 76.5 us
    pallas_call x1, Pallas kernels: 87.7 us -> 76.5 us  [on_device(): pl.pallas_call(functools.partial(kernel, chips), out_shape=(jax.ShapeDtyp...]
where the time goes in v2:
time: 81.9 us; the launch traced here: 81.6 us
  Pallas kernels  76.5 us (93%)
  local copies, waits for them, and re-layouts  3.35 us (4%)
  other arithmetic  1.74 us (2%)
    pallas_call x1, Pallas kernels, on_device(): pl.pallas_call(functools.partial(kernel, chips), out_shape=(jax.ShapeDtyp...  76.5 us
    unnamed x6, local copies, waits for them, and re-layouts  3.35 us

profile of v2, /device:TPU:0, one launch (start us, length us, event | category | flops | bytes accessed | tf_op | source)
XLA Modules:
  0.0 81.6 jit_solution(12519347810466091295)
XLA Ops:
  0.0 0.0 copy-start
  0.0 1.6 %copy-done = bf16[1024,1024]{1,0:T(8,128)(2,1)S(1)} copy-done((bf16[1024,1024]{1,0:T(8,128)(2,1)S(1)}, bf16[1024,1024]{1,0:T(8,128)(2,1)}, u32[]{:S(2)}) %copy-start) | copy-done | bytes 2097176
  1.6 0.0 copy-start.1
  1.6 1.0 %copy-done.1 = bf16[512,512]{1,0:T(8,128)(2,1)S(1)} copy-done((bf16[512,512]{1,0:T(8,128)(2,1)S(1)}, bf16[512,512]{1,0:T(8,128)(2,1)}, u32[]{:S(2)}) %copy-start.1) | copy-done | bytes 524312
  2.6 0.0 copy-start.2
  2.6 0.7 copy-done.2
  3.4 76.5 %shard_map.46 = (f32[1024,512]{1,0:T(8,128)S(1)}, f32[1024,128]{1,0:T(8,128)S(1)}) custom-call(bf16[1024,1024]{1,0:T(8,128)(2,1)S(1)} %copy-done, bf16[512,512]{1,0:T(8,128)(2,1)S(1)} %copy-done.1, f32[1024,512]{1,0:T(8,128)} %result_hbm.1, f32[1,4096]{1,0:T(1,128)S(1)} %bitcast.1), custom_call_target="tpu_custom_call" | custom-call | flops 4294967296 | bytes 8388608 | tf_op jit(solution)/shard_map/pallas_call | solution.py:294
  79.9 0.2 rsqrt_reduce_fusion
  80.1 1.5 %broadcast_multiply_fusion = f32[1024,512]{1,0:T(8,128)} fusion(f32[1024,512]{1,0:T(8,128)S(1)} %get-tuple-element.7, f32[1024]{0:T(1024)S(1)} %rsqrt_reduce_fusion), kind=kLoop, calls=%fused_computation | loop fusion | flops 524288 | bytes 4198400 | tf_op jit(solution)/shard_map/mul | solution.py:332
Async XLA Ops:
  0.0 1.6 %copy-start = (bf16[1024,1024]{1,0:T(8,128)(2,1)S(1)}, bf16[1024,1024]{1,0:T(8,128)(2,1)}, u32[]{:S(2)}) copy-start(bf16[1024,1024]{1,0:T(8,128)(2,1)} %left_hbm.1) | copy-start | bytes 6291460
  1.6 1.0 %copy-start.1 = (bf16[512,512]{1,0:T(8,128)(2,1)S(1)}, bf16[512,512]{1,0:T(8,128)(2,1)}, u32[]{:S(2)}) copy-start(bf16[512,512]{1,0:T(8,128)(2,1)} %right_hbm.1) | copy-start | bytes 1572868
  2.6 0.7 copy-start.2

commit v3 on v2

--- a/solution.py
+++ b/solution.py
@@ -9,10 +9,7 @@
 
 MESH = pl.DeviceIdType.MESH
 PIECES = 4
-TILES = 4
-SWAP = 0
-EARLY = 1
-VMEM = 48 * 1024 * 1024
+TILES = 2
 
 
 def gathered(first_factor, second_factor, result_in, pivot_scale):
@@ -39,8 +36,6 @@
     y, x = lane // 2, lane % 2
     peer = (2 * z + 1 - core, lane)
     lane_x, lane_y, lane_d = 2 * y + 1 - x, 2 * (1 - y) + x, 2 * (1 - y) + 1 - x
-    if SWAP:
-        lane_x, lane_y = lane_y, lane_x
     above, below = (band + 2, lane), (band - 2, lane)
     depth, width = right_hbm.shape
     half = width // 2
@@ -73,8 +68,6 @@
         return right.at[slot, pl.ds(start, piece), :]
 
     dx, dy = (x + z % 2) % 2, (y + z // 2) % 2
-    if SWAP:
-        dx, dy = dy, dx
     slot_0 = dx * (1 - dy) + 6 * (1 - dx) * dy + 4 * dx * dy
     slot_1 = 7 * (1 - dx) * (1 - dy) + 5 * dx * (1 - dy) + 3 * (1 - dx) * dy + 2 * dx * dy
 
@@ -182,6 +175,7 @@
 
         each_tile(body)
 
+    forward(0)
     load_left.wait()
     part_scale = scale_ref[:, pl.ds(pl.multiple_of(lane * share, share), share)]
 
@@ -190,7 +184,6 @@
 
     each_tile(scale_tile)
 
-    forward(0)
     await_peer(0)
     load_result.wait()
     multiply_own(0, 0)
@@ -213,16 +206,10 @@
     await_peer(6)
     multiply_keep(6, 1)
     combine_send(0, 1, 4, lane_x)
-    if EARLY:
-        combine_send(1, 0, 5, lane_y)
-        forward(7)
-        await_peer(7)
-        multiply_own(7, 1)
-    else:
-        forward(7)
-        combine_send(1, 0, 5, lane_y)
-        await_peer(7)
-        multiply_own(7, 1)
+    combine_send(1, 0, 5, lane_y)
+    forward(7)
+    await_peer(7)
+    multiply_own(7, 1)
 
     def finish(at, span):
         for buffer in (2, 3, 4, 5):
@@ -297,8 +284,12 @@
             jax.ShapeDtypeStruct((rows, width), jnp.float32),
             jax.ShapeDtypeStruct((rows, 128), jnp.float32),
         ),
-        in_specs=[pl.BlockSpec(memory_space=pl.ANY)] * 3
-        + [pl.BlockSpec(memory_space=pltpu.VMEM)],
+        in_specs=[
+            pl.BlockSpec(memory_space=pltpu.HBM),
+            pl.BlockSpec(memory_space=pl.ANY),
+            pl.BlockSpec(memory_space=pl.ANY),
+            pl.BlockSpec(memory_space=pltpu.VMEM),
+        ],
         out_specs=[pl.BlockSpec(memory_space=pltpu.VMEM)] * 2,
         scratch_shapes=[
             pltpu.VMEM((rows, share), jnp.bfloat16),
@@ -323,7 +314,7 @@
             dma((3,)),
         ],
         compiler_params=pltpu.CompilerParams(
-            collective_id=0, has_side_effects=True, vmem_limit_bytes=VMEM
+            collective_id=0, has_side_effects=True, vmem_limit_bytes=48 * 1024 * 1024
         ),
         cost_estimate=pl.CostEstimate(
             flops=flops, bytes_accessed=8 * rows * share, transcendentals=0

time: 81.9 us -> 80.7 us (0.985)
  Pallas kernels: 76.5 us -> 75.4 us
    pallas_call x1, Pallas kernels: 76.5 us -> 75.4 us  [on_device(): pl.pallas_call(functools.partial(kernel, chips), out_shape=(jax.ShapeDtyp...]
where the time goes in v3:
time: 80.7 us; the launch traced here: 80.5 us
  Pallas kernels  75.4 us (93%)
  local copies, waits for them, and re-layouts  3.35 us (4%)
  other arithmetic  1.74 us (2%)
    pallas_call x1, Pallas kernels, on_device(): pl.pallas_call(functools.partial(kernel, chips), out_shape=(jax.ShapeDtyp...  75.4 us
    unnamed x6, local copies, waits for them, and re-layouts  3.35 us

profile of v3, /device:TPU:0, one launch (start us, length us, event | category | flops | bytes accessed | tf_op | source)
XLA Modules:
  0.0 80.5 jit_solution(17103007908420895798)
XLA Ops:
  0.0 0.0 copy-start
  0.0 1.6 %copy-done = bf16[1024,1024]{1,0:T(8,128)(2,1)S(1)} copy-done((bf16[1024,1024]{1,0:T(8,128)(2,1)S(1)}, bf16[1024,1024]{1,0:T(8,128)(2,1)}, u32[]{:S(2)}) %copy-start) | copy-done | bytes 2097176
  1.6 0.0 copy-start.1
  1.6 1.0 %copy-done.1 = bf16[512,512]{1,0:T(8,128)(2,1)S(1)} copy-done((bf16[512,512]{1,0:T(8,128)(2,1)S(1)}, bf16[512,512]{1,0:T(8,128)(2,1)}, u32[]{:S(2)}) %copy-start.1) | copy-done | bytes 524312
  2.6 0.0 copy-start.2
  2.6 0.7 copy-done.2
  3.4 75.4 %shard_map.46 = (f32[1024,512]{1,0:T(8,128)S(1)}, f32[1024,128]{1,0:T(8,128)S(1)}) custom-call(bf16[1024,1024]{1,0:T(8,128)(2,1)S(1)} %copy-done, bf16[512,512]{1,0:T(8,128)(2,1)S(1)} %copy-done.1, f32[1024,512]{1,0:T(8,128)} %result_hbm.1, f32[1,4096]{1,0:T(1,128)S(1)} %bitcast.1), custom_call_target="tpu_custom_call" | custom-call | flops 4294967296 | bytes 8388608 | tf_op jit(solution)/shard_map/pallas_call | solution.py:281
  78.8 0.2 rsqrt_reduce_fusion
  79.0 1.5 %broadcast_multiply_fusion = f32[1024,512]{1,0:T(8,128)} fusion(f32[1024,512]{1,0:T(8,128)S(1)} %get-tuple-element.7, f32[1024]{0:T(1024)S(1)} %rsqrt_reduce_fusion), kind=kLoop, calls=%fused_computation | loop fusion | flops 524288 | bytes 4198400 | tf_op jit(solution)/shard_map/mul | solution.py:323
Async XLA Ops:
  0.0 1.6 %copy-start = (bf16[1024,1024]{1,0:T(8,128)(2,1)S(1)}, bf16[1024,1024]{1,0:T(8,128)(2,1)}, u32[]{:S(2)}) copy-start(bf16[1024,1024]{1,0:T(8,128)(2,1)} %left_hbm.1) | copy-start | bytes 6291460
  1.6 1.0 %copy-start.1 = (bf16[512,512]{1,0:T(8,128)(2,1)S(1)}, bf16[512,512]{1,0:T(8,128)(2,1)}, u32[]{:S(2)}) copy-start(bf16[512,512]{1,0:T(8,128)(2,1)} %right_hbm.1) | copy-start | bytes 1572868
  2.6 0.7 copy-start.2
